TPU v7x, 8 devices: a whole 2x2x1 slice. The times are simulated.
8 devices in a mesh: dp: 1 (over z), ep: 8 (over x, y, core).
Axes of the slice: x: 2, y: 2, z: 1, core: 2. Of those that a mesh axis runs over, the one named last changes fastest.
Arguments:
- x: bfloat16 [1, 8, 256, 5120], P('dp', 'ep')
- expert: int32 [1, 8, 256, 6], P('dp', 'ep')
- slot: int32 [1, 8, 256, 6], P('dp', 'ep')
- gate: float32 [1, 8, 256, 6], P('dp', 'ep')
- w_gate: bfloat16 [40, 5120, 1536], P('ep')
- w_up: bfloat16 [40, 5120, 1536], P('ep')
- w_down: bfloat16 [40, 1536, 5120], P('ep')
- s_gate: bfloat16 [5120, 3072], replicated
- s_up: bfloat16 [5120, 3072], replicated
- s_down: bfloat16 [3072, 5120], replicated
Outputs:
- y: bfloat16 [1, 8, 256, 5120], P('dp', 'ep')
All inputs are finite; a program needn't handle non-finite values.
Results may differ from a plain program's by a relative error of at most 0.009.
Values are sent between devices in bfloat16 or wider.
A program may use at most 2 GiB of HBM per device.

v0:
```python
import jax
import jax.numpy as jnp
from jax import lax
from jax.sharding import NamedSharding, PartitionSpec as P


def einsum(form, a, b):
    return jnp.einsum(form, a.astype(jnp.float32), b.astype(jnp.float32))


def for_all(x, s_gate, s_up, s_down):
    h = jax.nn.silu(einsum("...d,df->...f", x, s_gate)) * einsum("...d,df->...f", x, s_up)
    return einsum("...f,fd->...d", h.astype(jnp.bfloat16), s_down)


def solution(mesh):
    def placed(v, *spec):
        return lax.with_sharding_constraint(v, NamedSharding(mesh, P(*spec)))

    def step(x, expert, slot, gate, w_gate, w_up, w_down, s_gate, s_up, s_down):
        experts, (tokens, top) = w_gate.shape[0], expert.shape[2:]
        slots = 5 * tokens * top // (4 * experts)
        to_expert = jax.nn.one_hot(expert, experts, dtype=jnp.bfloat16)
        to_slot = jax.nn.one_hot(slot, slots, dtype=jnp.bfloat16)
        weighted = to_expert * gate[..., None].astype(jnp.bfloat16)
        dispatch = einsum("abtke,abtkc->abtec", to_expert, to_slot).astype(jnp.bfloat16)
        combine = einsum("abtke,abtkc->abtec", weighted, to_slot).astype(jnp.bfloat16)
        z = einsum("abtec,abtd->aebcd", dispatch, x).astype(jnp.bfloat16)
        z = placed(z, "dp", None, "ep", None, None)
        z = placed(z, "dp", "ep", None, None, None)
        h = jax.nn.silu(einsum("aebcd,edf->aebcf", z, w_gate))
        h = (h * einsum("aebcd,edf->aebcf", z, w_up)).astype(jnp.bfloat16)
        out = einsum("aebcf,efd->aebcd", h, w_down).astype(jnp.bfloat16)
        out = placed(out, "dp", "ep", None, None, None)
        out = placed(out, "dp", None, "ep", None, None)
        y = einsum("abtec,aebcd->abtd", combine, out)
        return (y + for_all(x, s_gate, s_up, s_down)).astype(jnp.bfloat16)

    return step
```

profile of v0, /device:TPU:0, one launch (start us, length us, event | category | flops | bytes accessed | tf_op | source)
XLA Modules:
  0.0 617.4 jit_solution(14083700743287802750)
XLA Ops:
  0.0 0.0 copy-start
  0.0 1.0 copy.21
  1.0 0.0 copy-start.1
  1.0 0.8 copy.23
  1.8 0.0 copy-start.3
  1.9 2.9 convolution_convert_fusion.1
  4.8 0.0 copy-done
  4.8 9.6 %convolution_convert_fusion = bf16[40,48,5120]{2,1,0:T(8,128)(2,1)} fusion(bf16[1,1,256,5120]{3,2,1,0:T(8,128)(2,1)S(1)} %copy-done, bf16[256,40,48]{2,1,0:T(8,128)(2,1)S(1)} %convolution_convert_fusion.1), kind=kOutput, calls=%fused_computation.11 | convolution fusion | flops 5042995200 | bytes 23265280 | tf_op jit(solution)/abtec,abtd->aebcd/dot_general | solution.py:8
  14.4 0.0 copy-done.1
  14.4 0.0 copy-done.3
  14.4 222.0 %all-to-all.4 = bf16[1,8,5,1,48,5120]{5,4,2,3,0,1:T(8,128)(2,1)} all-to-all(bf16[1,8,5,1,48,5120]{5,4,2,3,0,1:T(8,128)(2,1)} %bitcast.133), channel_id=1, replica_groups=mesh['dp'=1,'ep'=8] {'ep'}, dimensions={1} | all-to-all | bytes 39321600 | tf_op jit(solution)/sharding_constraint;jit(solution)/sharding_constraint | solution.py:18
  236.4 43.5 %fusion.4 = f32[5,8,48,1536]{3,2,1,0:T(8,128)} fusion(bf16[5,5120,1536]{2,1,0:T(8,128)(2,1)} %param.4, bf16[1,8,5,1,48,5120]{5,4,2,3,0,1:T(8,128)(2,1)} %all-to-all.4), kind=kOutput, calls=%fused_computation.4 | convolution fusion | flops 30198988800 | bytes 110100480 | tf_op jit(solution)/aebcd,edf->aebcf/dot_general | solution.py:8
  279.8 43.6 %fusion.12 = bf16[1,5,8,48,1536]{4,3,2,1,0:T(8,128)(2,1)} fusion(f32[5,8,48,1536]{3,2,1,0:T(8,128)} %fusion.4, bf16[5,5120,1536]{2,1,0:T(8,128)(2,1)} %param.5, bf16[1,8,5,1,48,5120]{5,4,2,3,0,1:T(8,128)(2,1)} %all-to-all.4), kind=kOutput, calls=%fused_computation.13 | convolution fusion | flops 30216683520 | bytes 115998720 | tf_op jit(solution)/aebcd,edf->aebcf/dot_general | solution.py:8
  323.4 45.9 %convert_bitcast_fusion = bf16[1,5,8,1,48,5120]{5,4,2,1,3,0:T(8,128)(2,1)} fusion(bf16[5,1536,5120]{2,1,0:T(8,128)(2,1)} %param.6, bf16[1,5,8,48,1536]{4,3,2,1,0:T(8,128)(2,1)} %fusion.12), kind=kOutput, calls=%fused_computation.8 | convolution fusion | flops 30208819200 | bytes 104202240 | tf_op jit(solution)/aebcf,efd->aebcd/dot_general | solution.py:8
  369.3 16.3 %copy.15 = bf16[1,5,8,1,48,5120]{5,4,1,3,0,2:T(8,128)(2,1)} copy(bf16[1,5,8,1,48,5120]{5,4,2,1,3,0:T(8,128)(2,1)} %convert_bitcast_fusion) | data formatting | bytes 39321600 | tf_op jit(solution)/sharding_constraint;jit(solution)/sharding_constraint | solution.py:18
  385.6 5.1 all-to-all-start.1
  390.7 0.0 copy-done.5
  390.8 0.1 copy.22
  390.9 0.0 copy-done.2
  390.9 4.2 convolution_convert_fusion.2
  395.2 16.0 %convolution_bitcast_fusion.2 = f32[1,256,3072]{2,1,0:T(8,128)} fusion(bf16[5120,3072]{1,0:T(8,128)(2,1)} %param.7, bf16[1,1,256,5120]{3,2,1,0:T(8,128)(2,1)S(1)} %copy-done), kind=kOutput, calls=%fused_computation.26 | convolution fusion | flops 8053063680 | bytes 37224448 | tf_op jit(solution)/...d,df->...f/dot_general | solution.py:8
  411.1 30.1 %fusion.27 = f32[256,5120]{1,0:T(8,128)} fusion(bf16[3072,5120]{1,0:T(8,128)(2,1)} %param.9, bf16[5120,3072]{1,0:T(8,128)(2,1)} %param.8, f32[1,256,3072]{2,1,0:T(8,128)} %convolution_bitcast_fusion.2, bf16[1,1,256,5120]{3,2,1,0:T(8,128)(2,1)S(1)} %copy-done), kind=kOutput, calls=%fused_computation.29 | convolution fusion | flops 16110845952 | bytes 73924608 | tf_op jit(solution)/...f,fd->...d/dot_general | solution.py:8
  441.2 163.0 %all-to-all-done.1 = bf16[1,5,8,1,48,5120]{5,4,1,3,0,2:T(8,128)(2,1)} async-done(((bf16[1,5,8,1,48,5120]{5,4,1,3,0,2:T(8,128)(2,1)}), bf16[1,5,8,1,48,5120]{5,4,1,3,0,2:T(8,128)(2,1)}, u32[]{:S(2)}, u32[]{:S(2)}) %all-to-all-start.1) | async-done | bytes 19660832 | tf_op jit(solution)/sharding_constraint;jit(solution)/sharding_constraint | solution.py:18
  604.3 13.2 %fusion.18 = bf16[1,1,256,5120]{3,2,1,0:T(8,128)(2,1)} fusion(f32[256,5120]{1,0:T(8,128)} %fusion.27, bf16[40,48,5120]{2,1,0:T(8,128)(2,1)} %bitcast.38, bf16[256,40,48]{2,1,0:T(8,128)(2,1)} %convolution_convert_fusion.2), kind=kOutput, calls=%fused_computation.22 | convolution fusion | flops 5035786240 | bytes 28508160 | tf_op jit(solution)/abtec,aebcd->abtd/dot_general | solution.py:8
  (5 shorter events, 0.0 us)
Async XLA Ops:
  0.0 4.8 copy-start
  1.0 13.4 %copy-start.1 = (s32[1,1,256,6]{3,2,1,0:T(8,128)}, s32[1,1,256,6]{3,2,1,0:T(8,128)S(1)}, u32[]{:S(2)}) copy-start(s32[1,1,256,6]{3,2,1,0:T(8,128)S(1)} %copy.21) | copy-start | bytes 18436
  1.8 12.5 %copy-start.3 = (s32[1,1,256,6]{3,2,1,0:T(8,128)}, s32[1,1,256,6]{3,2,1,0:T(8,128)S(1)}, u32[]{:S(2)}) copy-start(s32[1,1,256,6]{3,2,1,0:T(8,128)S(1)} %copy.23) | copy-start | bytes 18436
  385.6 5.1 copy-start.5
  385.6 5.3 copy-start.2
  385.6 5.3 copy-start.4
  385.6 218.6 %all-to-all-start.1 = ((bf16[1,5,8,1,48,5120]{5,4,1,3,0,2:T(8,128)(2,1)}), bf16[1,5,8,1,48,5120]{5,4,1,3,0,2:T(8,128)(2,1)}, u32[]{:S(2)}, u32[]{:S(2)}) async-start(bf16[1,5,8,1,48,5120]{5,4,1,3,0,2:T(8,128)(2,1)} %copy.15), calls=%async_computation.1 | async-start | bytes 39321600 | tf_op jit(solution)/sharding_constraint;jit(solution)/sharding_constraint | solution.py:18
where the time goes:
time: 618 us; the launch traced here: 617 us
  blocking collectives  222 us (36%)
  matrix products  209 us (34%)
  waiting for transfers between devices  163 us (26%)
  local copies, waits for them, and re-layouts  18.3 us (3%)
    another operation x1, blocking collectives, placed(): return lax.with_sharding_constraint(v, NamedSharding(mesh, P(*spec)))  222 us
    dot_general x9, matrix products, einsum(): return jnp.einsum(form, a.astype(jnp.float32), b.astype(jnp.float32))  209 us
    another operation x1, waiting for transfers between devices, placed(): return lax.with_sharding_constraint(v, NamedSharding(mesh, P(*spec)))  163 us
    another operation x1, local copies, waits for them, and re-layouts, placed(): return lax.with_sharding_constraint(v, NamedSharding(mesh, P(*spec)))  16.3 us
  transfers between devices with their start and end apart: 1, of which 1 were waited for; matrix products, arithmetic and copies ran while one was open for 8% of the time, Pallas kernels for 0%

commit v1 on v0

v1 whole, which is shorter than its diff:
```python
import jax
import jax.numpy as jnp
from jax import lax
from jax.sharding import PartitionSpec as P


def mm(form, a, b):
    return jnp.einsum(form, a, b, preferred_element_type=jnp.float32)


def solution(mesh):
    members = mesh.shape["ep"]

    def body(x, expert, slot, gate, w_gate, w_up, w_down, s_gate, s_up, s_down):
        x, expert, slot, gate = x[0, 0], expert[0, 0], slot[0, 0], gate[0, 0]
        local, depth, width = w_gate.shape
        tokens, top = expert.shape
        slots = 5 * tokens * top // (4 * members * local)
        rows = local * slots
        code = jnp.where(slot < slots, expert * slots + slot, -1)
        xs = lax.all_gather(x, "ep")
        codes = lax.all_gather(code, "ep") - lax.axis_index("ep") * rows
        gates = lax.all_gather(gate.astype(jnp.bfloat16), "ep")
        row = jnp.arange(rows, dtype=jnp.int32)
        hit = codes[..., None] == row
        dispatch = jnp.any(hit, axis=2).astype(jnp.bfloat16)
        combine = jnp.sum(jnp.where(hit, gates[..., None], 0), axis=2, dtype=jnp.bfloat16)
        z = mm("str,std->srd", dispatch, xs).astype(jnp.bfloat16)
        z = z.reshape(members, local, slots, depth).transpose(1, 0, 2, 3).reshape(local, members * slots, depth)
        h = jax.nn.silu(mm("ecd,edf->ecf", z, w_gate)) * mm("ecd,edf->ecf", z, w_up)
        out = mm("ecf,efd->ecd", h.astype(jnp.bfloat16), w_down).astype(jnp.bfloat16)
        out = out.reshape(local, members, slots, depth).transpose(1, 0, 2, 3).reshape(members, rows, depth)
        y = mm("str,srd->std", combine, out).astype(jnp.bfloat16)
        y = lax.psum_scatter(y, "ep", scatter_dimension=0)
        h = jax.nn.silu(mm("td,df->tf", x, s_gate)) * mm("td,df->tf", x, s_up)
        shared = mm("tf,fd->td", h.astype(jnp.bfloat16), s_down)
        return (y.astype(jnp.float32) + shared).astype(jnp.bfloat16)[None, None]

    own = P("dp", "ep", None, None)
    experts, whole = P("ep", None, None), P(None, None)
    return jax.shard_map(
        body,
        mesh=mesh,
        in_specs=(own, own, own, own, experts, experts, experts, whole, whole, whole),
        out_specs=own,
        check_vma=False,
    )
```

time: 618 us -> 486 us (0.79)
  blocking collectives: 222 us -> 25.5 us
  waiting for transfers between devices: 163 us -> 184 us
  local copies, waits for them, and re-layouts: 18.3 us -> 35.3 us
  between operations: 0.09 us -> 13.4 us
  matrix products: 209 us -> 220 us
  other arithmetic: 0.01 us -> 7.09 us
    another operation x1 -> x0, blocking collectives: 222 us -> none  [placed(): return lax.with_sharding_constraint(v, NamedSharding(mesh, P(*spec)))]
    another operation x1 -> x0, waiting for transfers between devices: 163 us -> none  [placed(): return lax.with_sharding_constraint(v, NamedSharding(mesh, P(*spec)))]
    reduce_scatter x0 -> x1, waiting for transfers between devices: none -> 109 us  [body(): y = lax.psum_scatter(y, 'ep', scatter_dimension=0)]
    all_gather x0 -> x1, waiting for transfers between devices: none -> 73.9 us  [body(): xs = lax.all_gather(x, 'ep')]
    transpose x0 -> x2, local copies, waits for them, and re-layouts: none -> 32.9 us  [the longest x1 16.5 us: body(): out.reshape(local, members, slots, depth).transpose(1, 0, 2, 3)]
    all_gather x0 -> x2, blocking collectives: none -> 25.5 us  [the longest x1 13.8 us: body(): codes = lax.all_gather(code, 'ep') - lax.axis_index('ep') * rows]
    another operation x1 -> x0, local copies, waits for them, and re-layouts: 16.3 us -> none  [placed(): return lax.with_sharding_constraint(v, NamedSharding(mesh, P(*spec)))]
    dot_general x9 -> x7, matrix products: 209 us -> 220 us  [mm(): return jnp.einsum(form, a, b, preferred_element_type=jnp.float32)]
  transfers between devices with their start and end apart: 1 -> 2, of which waited for: 1 -> 2; matrix products, arithmetic and copies ran while one was open for 8% -> 5% of each run, Pallas kernels for 0% -> 0%
where the time goes in v1:
time: 486 us
  matrix products  220 us (45%)
  waiting for transfers between devices  184 us (38%)
  local copies, waits for them, and re-layouts  35.3 us (7%)
  blocking collectives  25.5 us (5%)
  between operations  13.4 us (3%)
  other arithmetic  7.09 us (1%)
    dot_general x7, matrix products, mm(): return jnp.einsum(form, a, b, preferred_element_type=jnp.float32)  220 us
    reduce_scatter x1, waiting for transfers between devices, body(): y = lax.psum_scatter(y, 'ep', scatter_dimension=0)  109 us
    all_gather x1, waiting for transfers between devices, body(): xs = lax.all_gather(x, 'ep')  73.9 us
    transpose x1, local copies, waits for them, and re-layouts, body(): out.reshape(local, members, slots, depth).transpose(1, 0, 2, 3)  16.5 us
    transpose x1, local copies, waits for them, and re-layouts, body(): z.reshape(members, local, slots, depth).transpose(1, 0, 2, 3)  16.4 us
    all_gather x1, blocking collectives, body(): codes = lax.all_gather(code, 'ep') - lax.axis_index('ep') * rows  13.8 us
    all_gather x1, blocking collectives, body(): gates = lax.all_gather(gate.astype(jnp.bfloat16), 'ep')  11.6 us
  transfers between devices with their start and end apart: 2, of which 2 were waited for; matrix products, arithmetic and copies ran while one was open for 5% of the time, Pallas kernels for 0%

profile of v1, /device:TPU:0, one launch (start us, length us, event | category | flops | bytes accessed | tf_op | source)
XLA Modules:
  0.0 485.8 jit_solution(12509906969764192424)
XLA Ops:
  6.5 0.0 all-gather.5.cloned.1.call-start
  6.5 0.7 all-gather.5.cloned.1.call-update
  7.3 0.0 reduce-scatter.2.cloned.1.call-start
  7.3 0.7 compare_select_fusion
  8.0 13.8 %all-gather = s32[8,1,256,6]{2,1,3,0:T(1,128)S(1)} all-gather(s32[1,1,256,6]{2,1,3,0:T(1,128)S(1)} %compare_select_fusion), channel_id=2, replica_groups=mesh['dp'=1,'ep'=8] {'ep'}, dimensions={0}, use_global_device_ids=true | all-gather | bytes 55296 | tf_op jit(solution)/shard_map/all_gather | solution.py:22
  21.9 0.7 copy.46
  22.6 11.6 %all-gather.1 = bf16[8,1,256,6]{2,3,1,0:T(8,128)(2,1)S(1)} all-gather(bf16[1,1,256,6]{2,3,1,0:T(8,128)(2,1)S(1)} %copy.46), channel_id=3, replica_groups=mesh['dp'=1,'ep'=8] {'ep'}, dimensions={0}, use_global_device_ids=true | all-gather | bytes 27648 | tf_op jit(solution)/shard_map/all_gather | solution.py:23
  34.3 3.2 fusion.5
  37.5 3.2 fusion.9
  40.6 73.9 %all-gather.5.cloned.1.call-done = bf16[8,1,256,5120]{3,2,1,0:T(8,128)(2,1)} async-done(((bf16[1,1,256,5120]{3,2,1,0:T(8,128)(2,1)}), bf16[8,1,256,5120]{3,2,1,0:T(8,128)(2,1)}) %all-gather.5.cloned.1.call-update) | async-done | bytes 20971536 | tf_op jit(solution)/shard_map/all_gather | solution.py:21
  114.6 20.8 %fusion.2 = bf16[8,240,5120]{2,1,0:T(8,128)(2,1)} fusion(pred[8,256,240]{1,2,0:T(8,128)(4,1)S(1)} %fusion.5, bf16[8,1,256,5120]{3,2,1,0:T(8,128)(2,1)} %all-gather.5.cloned.1.call-done), kind=kOutput, calls=%fused_computation.4 | convolution fusion | flops 5042995200 | bytes 41123840 | tf_op jit(solution)/shard_map/str,std->srd/dot_general | solution.py:8
  135.4 16.4 %copy.39 = bf16[5,8,48,5120]{3,2,1,0:T(8,128)(2,1)} copy(bf16[5,8,48,5120]{3,2,0,1:T(8,128)(2,1)} %bitcast.40) | data formatting | bytes 39321600 | tf_op jit(solution)/shard_map/transpose | solution.py:29
  151.8 43.4 %fusion.25 = f32[5,384,1536]{2,1,0:T(8,128)} fusion(bf16[5,384,5120]{2,1,0:T(8,128)(2,1)} %bitcast.41, bf16[5,5120,1536]{2,1,0:T(8,128)(2,1)} %param.14), kind=kOutput, calls=%fused_computation.31 | convolution fusion | flops 30198988800 | bytes 110100480 | tf_op jit(solution)/shard_map/ecd,edf->ecf/dot_general | solution.py:8
  195.2 44.0 %fusion.26 = f32[5,384,1536]{2,1,0:T(8,128)} fusion(bf16[5,384,5120]{2,1,0:T(8,128)(2,1)} %bitcast.42, bf16[5,5120,1536]{2,1,0:T(8,128)(2,1)} %param.15), kind=kOutput, calls=%fused_computation.32 | convolution fusion | flops 30198988800 | bytes 110100480 | tf_op jit(solution)/shard_map/ecd,edf->ecf/dot_general | solution.py:8
  239.2 47.2 %convolution_convert_fusion.1 = bf16[5,384,5120]{2,1,0:T(8,128)(2,1)} fusion(bf16[5,1536,5120]{2,1,0:T(8,128)(2,1)} %param.16, f32[5,384,1536]{2,1,0:T(8,128)} %fusion.26, f32[5,384,1536]{2,1,0:T(8,128)} %fusion.25), kind=kOutput, calls=%fused_computation.3 | convolution fusion | flops 30226513920 | bytes 121896960 | tf_op jit(solution)/shard_map/ecf,efd->ecd/dot_general | solution.py:8
  286.4 0.0 copy-start
  286.4 16.5 %copy.40 = bf16[8,5,48,5120]{3,2,1,0:T(8,128)(2,1)} copy(bf16[8,5,48,5120]{3,2,0,1:T(8,128)(2,1)} %bitcast.43) | data formatting | bytes 39321600 | tf_op jit(solution)/shard_map/transpose | solution.py:32
  302.9 0.0 copy-done
  302.9 18.3 %convolution_convert_fusion = bf16[8,256,5120]{2,1,0:T(8,128)(2,1)} fusion(bf16[8,256,240]{1,2,0:T(8,128)(2,1)S(1)} %copy-done, bf16[8,240,5120]{2,1,0:T(8,128)(2,1)} %bitcast.39), kind=kOutput, calls=%fused_computation.2 | convolution fusion | flops 5043650560 | bytes 41615360 | tf_op jit(solution)/shard_map/str,srd->std/dot_general | solution.py:8
  321.3 0.0 reduce-scatter.2.cloned.1.call-update
  321.3 1.7 copy-done.1
  323.0 15.9 %fusion.19 = f32[256,3072]{1,0:T(8,128)} fusion(bf16[5120,3072]{1,0:T(8,128)(2,1)} %param.17, bf16[1,1,256,5120]{3,2,1,0:T(8,128)(2,1)S(1)} %copy-done.1), kind=kOutput, calls=%fused_computation.22 | convolution fusion | flops 8053063680 | bytes 37224448 | tf_op jit(solution)/shard_map/td,df->tf/dot_general | solution.py:8
  338.9 109.4 %reduce-scatter.2.cloned.1.call-done = bf16[1,256,5120]{2,1,0:T(8,128)(2,1)} async-done(((bf16[8,256,5120]{2,1,0:T(8,128)(2,1)}), bf16[1,256,5120]{2,1,0:T(8,128)(2,1)}) %reduce-scatter.2.cloned.1.call-update) | async-done | bytes 2621456 | tf_op jit(solution)/shard_map/reduce_scatter | solution.py:34
  448.3 30.7 %fusion.8 = bf16[1,1,256,5120]{3,2,1,0:T(8,128)(2,1)} fusion(bf16[3072,5120]{1,0:T(8,128)(2,1)} %param.19, bf16[5120,3072]{1,0:T(8,128)(2,1)} %param.18, f32[256,3072]{1,0:T(8,128)} %fusion.19, bf16[1,256,5120]{2,1,0:T(8,128)(2,1)} %reduce-scatter.2.cloned.1.call-done, bf16[1,1,256,5120]{3,2,1,0:T(8,128)(2,1)S(1)} %copy-done.1), kind=kOutput, calls=%fused_computation.11 | convolution fusion | flops 16114778112 | bytes 73924608 | tf_op jit(solution)/shard_map/tf,fd->td/dot_general | solution.py:8
  (3 shorter events, 0.0 us)
Async XLA Ops:
  6.5 108.0 %all-gather.5.cloned.1.call-start = ((), (), s32[]{:S(2)}) async-start(), calls=%async_computation.2 | async-start | bytes 23592960 | tf_op jit(solution)/shard_map/all_gather | solution.py:21
  7.3 441.0 %reduce-scatter.2.cloned.1.call-start = ((), (), s32[]{:S(2)}) async-start(), calls=%async_computation.1 | async-start | bytes 23592960 | tf_op jit(solution)/shard_map/reduce_scatter | solution.py:34
  286.4 16.5 %copy-start = (bf16[8,256,240]{1,2,0:T(8,128)(2,1)S(1)}, bf16[8,256,240]{1,2,0:T(8,128)(2,1)}, u32[]{:S(2)}) copy-start(bf16[8,256,240]{1,2,0:T(8,128)(2,1)} %fusion.9) | copy-start | bytes 2949124
  321.3 1.7 copy-start.1
Sparse Core Ops, SparseCore 0:
  9.1 105.3 all-gather.4
  321.4 126.8 reduce-scatter.1

commit v2 on v1

v2 whole, which is shorter than its diff:
```python
import functools

import jax
import jax.numpy as jnp
from jax import lax
from jax.experimental import pallas as pl
from jax.experimental.pallas import tpu as pltpu
from jax.sharding import PartitionSpec as P

F32, BF16 = jnp.float32, jnp.bfloat16
MESH = pl.DeviceIdType.MESH
C = 512
UNITS = 8


def dot(a, b):
    return jnp.dot(a, b, preferred_element_type=F32)


def moe_kernel(
    dims, pk, x, wg, wu, wd, sg, su, sd, y,
    xg, acc, ring, hs, zb, dm, wm, cg,
    ld_sem, cg_send, cg_recv, ag_send, ag_recv, ring_sem, rs_send, rs_recv, out_sem,
):
    members, local, slots, top, chunks, parts = dims
    T = 256
    rows = local * slots
    M = members * slots
    K = chunks
    me = lax.axis_index("ep")
    core, yy, xx = me % 2, (me // 2) % 2, me // 4
    mate, ynbr, xnbr = me + 1 - 2 * core, me + 2 - 4 * yy, me + 4 - 8 * xx
    diag = ynbr + 4 - 8 * xx
    n_shared, n_routed, n_down = 4 * K, 2 * local * K, (local + 2) * K

    def unit_copy(src, r0, c0, down, n):
        slot = n % UNITS
        for j in range(parts):
            if down:
                piece = src.at[pl.ds(r0 + j * C, C), pl.ds(c0, C)]
            else:
                piece = src.at[pl.ds(r0, C), pl.ds(c0 + j * C, C)]
            pltpu.make_async_copy(piece, ring.at[slot, j], ring_sem.at[slot]).start()

    def unit_wait(n):
        slot = n % UNITS
        pltpu.make_async_copy(ring.at[slot], ring.at[slot], ring_sem.at[slot]).wait()
        return slot

    def start_shared(i, q, n):
        unit_copy(sg if q % 2 == 0 else su, pl.multiple_of(i * C, C), (q // 2) * parts * C, False, n)

    def start_routed(k, q, n):
        w = wg if q % 2 == 0 else wu
        unit_copy(w.at[q // 2], pl.multiple_of(k * C, C), 0, False, n)

    def start_down(k, m, n):
        c0 = pl.multiple_of(k * C, C)
        if m < local:
            unit_copy(wd.at[m], 0, c0, True, n)
        else:
            unit_copy(sd, (m - local) * parts * C, c0, True, n)

    def blk(k, s, off=0, n=T):
        return xg.at[k, pl.ds(pl.multiple_of(s * T + off, 128), n)]

    H = T // 2
    routes = (
        (me, 0, T, xnbr), (me, 0, T, ynbr), (me, 0, T, mate),
        (xnbr, 0, H, ynbr), (ynbr, H, H, xnbr),
        (xnbr, 0, T, mate), (ynbr, 0, T, mate), (diag, 0, H, mate), (diag, H, H, mate),
    )
    mx, my, md = mate + 4 - 8 * xx, mate + 2 - 4 * yy, mate + 2 - 4 * yy + 4 - 8 * xx
    landed = (
        (xnbr, 0, T), (ynbr, 0, T), (mate, 0, T), (diag, 0, H), (diag, H, H),
        (mx, 0, T), (my, 0, T), (md, 0, H), (md, H, H),
    )

    def route(kind, k, ref, dev):
        return pltpu.make_async_remote_copy(
            src_ref=ref, dst_ref=ref, send_sem=ag_send.at[kind, k], recv_sem=ag_recv.at[kind, k],
            device_id={"ep": dev}, device_id_type=MESH,
        )

    def ag_start(kinds, k):
        for kind in kinds:
            s, off, n, dev = routes[kind]
            route(kind, k, blk(k, s, off, n), dev).start()

    def ag_sent(kinds, k):
        for kind in kinds:
            s, off, n, dev = routes[kind]
            route(kind, k, blk(k, s, off, n), dev).wait_send()

    def ag_wait(kinds, k):
        for kind in kinds:
            s, off, n = landed[kind]
            route(kind, k, blk(k, s, off, n), mate).wait_recv()

    def comm_a(k):
        ag_wait((0, 1), k)

        @pl.when(k >= 2)
        def _():
            ag_sent(range(9), k - 2)

        ag_start((3, 4, 5, 6), k)

        @pl.when(k + 2 < K)
        def _():
            ag_start((0, 1, 2), k + 2)

    def comm_b(k):
        ag_wait((3, 4), k)
        ag_start((7, 8), k)

    def own_load(k):
        return pltpu.make_async_copy(x.at[:, pl.ds(pl.multiple_of(k * C, C), C)], blk(k, me), ld_sem.at[k])

    for k in range(K):
        own_load(k).start()
    for n in range(UNITS):
        start_shared(n // 4, n % 4, n)
    barrier = pltpu.get_barrier_semaphore()
    for d in range(1, members):
        pl.semaphore_signal(barrier, inc=1, device_id={"ep": (me + d) % members}, device_id_type=MESH)
    pl.semaphore_wait(barrier, members - 1)

    def code_copy(d, src, dst, dev):
        return pltpu.make_async_remote_copy(
            src_ref=src, dst_ref=dst, send_sem=cg_send.at[d], recv_sem=cg_recv.at[d],
            device_id={"ep": dev}, device_id_type=MESH,
        )

    own_load(0).wait()
    ag_start((0, 1, 2), 0)
    for d in range(1, members):
        code_copy(d, pk, cg.at[me], (me + d) % members).start()
    own_load(1).wait()
    ag_start((0, 1, 2), 1)
    cg[me] = pk[...]

    def shared_step(i, _):
        @pl.when(i >= 2)
        def _():
            own_load(i).wait()

        xo = blk(i, me)
        for half in range(2):
            for t in range(2):
                q = 2 * half + t
                n = 4 * i + q
                slot = unit_wait(n)
                for j in range(parts):
                    cols = pl.ds((t * parts + j) * C, C)
                    old = jnp.where(i > 0, acc[3 + half, :T, cols], 0.0)
                    acc[3 + half, :T, cols] = old + dot(xo[...], ring[slot, j])

                @pl.when(i < K - 2)
                def _():
                    start_shared(i + 2, q, n + UNITS)

                for late in range(2):
                    @pl.when(i == K - 2 + late)
                    def _():
                        start_routed(0, 4 * late + q, n + UNITS)

        @pl.when(i == 3)
        def _():
            comm_a(0)

        @pl.when(i == 7)
        def _():
            comm_a(1)
        return 0

    lax.fori_loop(0, K, shared_step, 0)
    for half in range(2):
        for j in range(parts):
            g = acc[3 + half, :T, pl.ds(j * C, C)]
            u = acc[3 + half, :T, pl.ds((parts + j) * C, C)]
            hs[half * parts + j] = (jax.nn.silu(g) * u).astype(BF16)

    zb[pl.ds(local * M, members * T - local * M)] = jnp.zeros((members * T - local * M, C), BF16)
    for d in range(1, members):
        code_copy(d, pk, cg.at[(me + members - d) % members], mate).wait_recv()

    def tables(s, _):
        codes = cg[s]
        row = lax.broadcasted_iota(jnp.int32, (T, T), 0)
        row = jnp.where(row < rows, row + me * rows, -2).astype(F32)
        hit = jnp.zeros((T, T), F32)
        weight = jnp.zeros((T, T), F32)
        for j in range(top):
            same = codes[j:j + 1, :] == row
            hit = jnp.where(same, 1.0, hit)
            weight = jnp.where(same, codes[8 + j:9 + j, :], weight)
        dm[s] = hit.astype(BF16)
        wm[s] = weight.T.astype(BF16)
        return 0

    lax.fori_loop(0, members, tables, 0)
    comm_b(0)

    def routed_step(k, _):
        ag_wait((2, 5, 6, 7, 8), k)
        for s in range(members):
            z = dot(dm[s, :rows], xg[k, pl.ds(s * T, T)]).astype(BF16)
            for e in range(local):
                zb[pl.ds(e * M + s * slots, slots)] = z[e * slots:(e + 1) * slots]

        def expert(e):
            z = zb[pl.ds(e * M, M)]
            for t in range(2):
                q = 2 * e + t
                n = n_shared + 2 * local * k + q
                slot = unit_wait(n)
                for j in range(parts):
                    cols = pl.ds((t * parts + j) * C, C)
                    old = jnp.where(k > 0, acc[e, :, cols], 0.0)
                    acc[e, :, cols] = old + dot(z, ring[slot, j])
                ahead = q + UNITS
                if ahead < 2 * local:
                    start_routed(k, ahead, n + UNITS)
                else:
                    ahead -= 2 * local

                    @pl.when(k + 1 < K)
                    def _():
                        start_routed(k + 1, ahead, n + UNITS)

                    @pl.when(k + 1 == K)
                    def _():
                        start_down(ahead // (local + 2), ahead % (local + 2), n + UNITS)

        for e in range(3):
            expert(e)

        @pl.when(k + 2 < K)
        def _():
            comm_a(k + 2)

        for e in range(3, local):
            expert(e)

        @pl.when(k + 1 < K)
        def _():
            comm_b(k + 1)
        return 0

    lax.fori_loop(0, K, routed_step, 0)
    for k in range(K - 2, K):
        ag_sent(range(9), k)

    for e in range(local):
        for j in range(parts):
            g = acc[e, :, pl.ds(j * C, C)]
            u = acc[e, :, pl.ds((parts + j) * C, C)]
            xg[6 + j, pl.ds(e * M, M)] = (jax.nn.silu(g) * u).astype(BF16)

    spans = ((0, T), (T, T), (2 * T, T), (3 * T, T), (4 * T, H), (4 * T + H, H), (5 * T, T), (6 * T, T))
    targets = (mate, mate, mate, mate, xnbr, ynbr, xnbr, ynbr)
    mine, theirs = (diag, xnbr, ynbr, me), (md, mx, my, mate)

    def rs_copy(kind, k):
        off, n = spans[kind]
        return pltpu.make_async_remote_copy(
            src_ref=xg.at[4 + k % 2, pl.ds(off, n)], dst_ref=xg.at[k % 4, pl.ds(off, n)],
            send_sem=rs_send.at[kind, k % 2], recv_sem=rs_recv.at[kind, k % 4],
            device_id={"ep": targets[kind]}, device_id_type=MESH,
        )

    def rs_free(kinds, k):
        @pl.when(k >= 2)
        def _():
            for kind in kinds:
                rs_copy(kind, k - 2).wait_send()

    def got(kind, k, lo=0, n=None):
        off, size = spans[kind]
        return xg[k % 4, pl.ds(off + lo, size if n is None else n)].astype(F32)

    def part(r, k):
        return acc.at[k % 4, pl.ds(0, T), pl.ds(r * C, C)]

    def compute(k):
        base = n_shared + n_routed + (local + 2) * k

        def refill(m):
            ahead = m + UNITS
            ks, ms = ahead // (local + 2), ahead % (local + 2)

            @pl.when(k + ks < K)
            def _():
                start_down(k + ks, ms, base + m + UNITS)

        for e in range(local):
            slot = unit_wait(base + e)
            out = dot(xg[6, pl.ds(e * M, M)], ring[slot, 0])
            for j in range(1, parts):
                out = out + dot(xg[6 + j, pl.ds(e * M, M)], ring[slot, j])
            out = out.astype(BF16)
            for s in range(members):
                zb[pl.ds(s * T + e * slots, slots)] = out[s * slots:(s + 1) * slots]
            refill(e)
        rs_free(range(4), k)
        for r in range(4):
            s = theirs[r]
            p = dot(wm[s], zb[pl.ds(pl.multiple_of(s * T, T), T)])
            xg[4 + k % 2, pl.ds(r * T, T)] = p.astype(BF16)
            rs_copy(r, k).start()
        for r in range(4):
            s = mine[r]
            part(r, k)[...] = dot(wm[s], zb[pl.ds(pl.multiple_of(s * T, T), T)])
        rs_copy(0, k).wait_recv()
        rs_free((4, 5), k)
        xg[4 + k % 2, pl.ds(4 * T, T)] = (part(0, k)[...] + got(0, k)).astype(BF16)
        rs_copy(4, k).start()
        rs_copy(5, k).start()
        total = None
        for half in range(2):
            slot = unit_wait(base + local + half)
            for j in range(parts):
                term = dot(hs[half * parts + j], ring[slot, j])
                total = term if total is None else total + term
            if half == 1:
                part(4, k)[...] = total
            refill(local + half)

    def pass_on(k):
        for kind in (1, 2, 4, 5):
            rs_copy(kind, k).wait_recv()
        rs_free((6, 7), k)
        out = xg.at[4 + k % 2]
        px, py = part(1, k), part(2, k)
        out[pl.ds(5 * T, H)] = (px[:H] + got(1, k, 0, H)).astype(BF16)
        out[pl.ds(5 * T + H, H)] = (px[H:] + got(1, k, H, H) + got(5, k)).astype(BF16)
        rs_copy(6, k).start()
        out[pl.ds(6 * T, H)] = (py[:H] + got(2, k, 0, H) + got(4, k)).astype(BF16)
        out[pl.ds(6 * T + H, H)] = (py[H:] + got(2, k, H, H)).astype(BF16)
        rs_copy(7, k).start()

    def out_copy(k):
        return pltpu.make_async_copy(
            xg.at[9, pl.ds((k % 2) * T, T)], y.at[:, pl.ds(pl.multiple_of(k * C, C), C)], out_sem.at[k % 2]
        )

    def finish(k):
        for kind in (3, 6, 7):
            rs_copy(kind, k).wait_recv()

        @pl.when(k >= 2)
        def _():
            out_copy(k - 2).wait()

        total = part(3, k)[...] + got(3, k) + got(6, k) + got(7, k) + part(4, k)[...]
        xg[9, pl.ds((k % 2) * T, T)] = total.astype(BF16)
        out_copy(k).start()

    def down_step(i, _):
        @pl.when(i < K)
        def _():
            compute(i)

        @pl.when((i >= 1) & (i <= K))
        def _():
            pass_on(i - 1)

        @pl.when(i >= 2)
        def _():
            finish(i - 2)
        return 0

    lax.fori_loop(0, K + 2, down_step, 0)
    for k in range(K - 2, K):
        out_copy(k).wait()
        for kind in range(8):
            rs_copy(kind, k).wait_send()
    for d in range(1, members):
        code_copy(d, pk, cg.at[me], mate).wait_send()


def solution(mesh):
    members = mesh.shape["ep"]

    def body(x, expert, slot, gate, w_gate, w_up, w_down, s_gate, s_up, s_down):
        x, expert, slot, gate = x[0, 0], expert[0, 0], slot[0, 0], gate[0, 0]
        local, depth, width = w_gate.shape
        tokens, top = expert.shape
        slots = 5 * tokens * top // (4 * members * local)
        code = jnp.where(slot < slots, expert * slots + slot, -1).astype(F32)
        weight = gate.astype(BF16).astype(F32)
        pad = jnp.zeros((8 - top, tokens), F32)
        pk = jnp.concatenate([code.T, pad, weight.T, pad])
        chunks, parts = depth // C, width // C
        dims = (members, local, slots, top, chunks, parts)
        rows, M = local * slots, members * slots
        anywhere = pl.BlockSpec(memory_space=pl.ANY)
        dma = pltpu.SemaphoreType.DMA
        out = pl.pallas_call(
            functools.partial(moe_kernel, dims),
            out_shape=jax.ShapeDtypeStruct((tokens, depth), BF16),
            in_specs=[pl.BlockSpec(memory_space=pltpu.VMEM)] + [anywhere] * 7,
            out_specs=anywhere,
            scratch_shapes=[
                pltpu.VMEM((chunks, members * tokens, C), BF16),
                pltpu.VMEM((local, M, 2 * width), F32),
                pltpu.VMEM((UNITS, parts, C, C), BF16),
                pltpu.VMEM((2 * parts, tokens, C), BF16),
                pltpu.VMEM((members * tokens, C), BF16),
                pltpu.VMEM((members, tokens, tokens), BF16),
                pltpu.VMEM((members, tokens, tokens), BF16),
                pltpu.VMEM((members, 16, tokens), F32),
                dma((chunks,)), dma((members,)), dma((members,)),
                dma((9, chunks)), dma((9, chunks)), dma((UNITS,)),
                dma((8, 2)), dma((8, 4)), dma((2,)),
            ],
            compiler_params=pltpu.CompilerParams(
                collective_id=0, has_side_effects=True, vmem_limit_bytes=67_000_000
            ),
            name="moe",
        )(pk, x, w_gate, w_up, w_down, s_gate, s_up, s_down)
        return out[None, None]

    own = P("dp", "ep", None, None)
    experts, whole = P("ep", None, None), P(None, None)
    return jax.shard_map(
        body,
        mesh=mesh,
        in_specs=(own, own, own, own, experts, experts, experts, whole, whole, whole),
        out_specs=own,
        check_vma=False,
    )
```

time: 486 us -> 240 us (0.49)
  Pallas kernels: 0 us -> 234 us
  matrix products: 220 us -> 0 us
  waiting for transfers between devices: 184 us -> 0 us
  local copies, waits for them, and re-layouts: 35.3 us -> 3.4 us
  blocking collectives: 25.5 us -> 0 us
  between operations: 13.4 us -> 0.01 us
  other arithmetic: 7.09 us -> 2.02 us
    pallas_call x0 -> x1, Pallas kernels: none -> 234 us  [body(): pl.pallas_call(functools.partial(moe_kernel, dims), out_shape=jax.ShapeDt...]
    dot_general x7 -> x0, matrix products: 220 us -> none  [mm(): return jnp.einsum(form, a, b, preferred_element_type=jnp.float32)]
    reduce_scatter x1 -> x0, waiting for transfers between devices: 109 us -> none  [body(): y = lax.psum_scatter(y, 'ep', scatter_dimension=0)]
    all_gather x1 -> x0, waiting for transfers between devices: 73.9 us -> none  [body(): xs = lax.all_gather(x, 'ep')]
    transpose x2 -> x0, local copies, waits for them, and re-layouts: 32.9 us -> none  [the longest x1 16.5 us: body(): out.reshape(local, members, slots, depth).transpose(1, 0, 2, 3)]
    all_gather x2 -> x0, blocking collectives: 25.5 us -> none  [the longest x1 13.8 us: body(): codes = lax.all_gather(code, 'ep') - lax.axis_index('ep') * rows]
  transfers between devices with their start and end apart: 2 -> 0, of which waited for: 2 -> 0; matrix products, arithmetic and copies ran while one was open for 5% -> 0% of each run, Pallas kernels for 0% -> 0%
where the time goes in v2:
time: 240 us; the launch traced here: 239 us
  Pallas kernels  234 us (98%)
  local copies, waits for them, and re-layouts  3.4 us (1%)
    pallas_call x1, Pallas kernels, body(): pl.pallas_call(functools.partial(moe_kernel, dims), out_shape=jax.ShapeDt...  234 us

profile of v2, /device:TPU:0, one launch (start us, length us, event | category | flops | bytes accessed | tf_op | source)
XLA Modules:
  0.0 239.5 jit_solution(9613405866622577724)
XLA Ops:
  0.0 0.7 fusion.2
  0.7 0.7 convert_bitcast_fusion
  1.4 0.6 pad_maximum_fusion.pk
  2.0 234.1 %moe.1 = bf16[256,5120]{1,0:T(8,128)(2,1)} custom-call(f32[16,256]{1,0:T(8,128)} %pad_maximum_fusion.pk, bf16[256,5120]{1,0:T(8,128)(2,1)} %bitcast.14, bf16[5,5120,1536]{2,1,0:T(8,128)(2,1)} %wg.1, bf16[5,5120,1536]{2,1,0:T(8,128)(2,1)} %wu.1, bf16[5,1536,5120]{2,1,0:T(8,128)(2,1)} %wd.1, bf16[5120,3072]{1,0:T(8,128)(2,1)} %sg.1, bf16[5120,3072]{1,0:T(8,128)(2,1)} %su.1, ...), custom_call_target="tpu_custom_call" | custom-call | tf_op jit(solution)/shard_map/moe/pallas_call | solution.py:400
  236.1 3.4 %copy.34 = bf16[1,1,256,5120]{3,2,1,0:T(8,128)(2,1)} copy(bf16[1,1,256,5120]{3,2,1,0:T(8,128)(2,1)} %bitcast.13) | data formatting | bytes 5242880
  (1 shorter events, 0.0 us)

commit v3 on v2

--- a/solution.py
+++ b/solution.py
@@ -18,8 +18,8 @@
 
 
 def moe_kernel(
-    dims, pk, x, wg, wu, wd, sg, su, sd, y,
-    xg, acc, ring, hs, zb, dm, wm, cg,
+    dims, expert, slot_of, gate, x, wg, wu, wd, sg, su, sd, y,
+    xg, acc, ring, hs, zb, dm, wm, cg, pk,
     ld_sem, cg_send, cg_recv, ag_send, ag_recv, ring_sem, rs_send, rs_recv, out_sem,
 ):
     members, local, slots, top, chunks, parts = dims
@@ -121,6 +121,11 @@
         own_load(k).start()
     for n in range(UNITS):
         start_shared(n // 4, n % 4, n)
+    pk[...] = jnp.zeros(pk.shape, F32)
+    for j in range(top):
+        place = slot_of[j]
+        pk[j:j + 1] = jnp.where(place < slots, expert[j] * slots + place, -1).astype(F32)
+        pk[8 + j:9 + j] = gate[j].astype(BF16).astype(F32)
     barrier = pltpu.get_barrier_semaphore()
     for d in range(1, members):
         pl.semaphore_signal(barrier, inc=1, device_id={"ep": (me + d) % members}, device_id_type=MESH)
@@ -140,30 +145,29 @@
     ag_start((0, 1, 2), 1)
     cg[me] = pk[...]
 
+    for k in range(2, K):
+        own_load(k).wait()
+
     def shared_step(i, _):
-        @pl.when(i >= 2)
-        def _():
-            own_load(i).wait()
-
         xo = blk(i, me)
+        held = [unit_wait(4 * i + q) for q in range(4)]
         for half in range(2):
             for t in range(2):
-                q = 2 * half + t
-                n = 4 * i + q
-                slot = unit_wait(n)
                 for j in range(parts):
                     cols = pl.ds((t * parts + j) * C, C)
                     old = jnp.where(i > 0, acc[3 + half, :T, cols], 0.0)
-                    acc[3 + half, :T, cols] = old + dot(xo[...], ring[slot, j])
-
-                @pl.when(i < K - 2)
-                def _():
-                    start_shared(i + 2, q, n + UNITS)
-
-                for late in range(2):
-                    @pl.when(i == K - 2 + late)
-                    def _():
-                        start_routed(0, 4 * late + q, n + UNITS)
+                    acc[3 + half, :T, cols] = old + dot(xo[...], ring[held[2 * half + t], j])
+
+        @pl.when(i < K - 2)
+        def _():
+            for q in range(4):
+                start_shared(i + 2, q, 4 * i + q + UNITS)
+
+        for late in range(2):
+            @pl.when(i == K - 2 + late)
+            def _():
+                for q in range(4):
+                    start_routed(0, 4 * late + q, 4 * i + q + UNITS)
 
         @pl.when(i == 3)
         def _():
@@ -202,61 +206,60 @@
     lax.fori_loop(0, members, tables, 0)
     comm_b(0)
 
-    def routed_step(k, _):
-        ag_wait((2, 5, 6, 7, 8), k)
-        for s in range(members):
-            z = dot(dm[s, :rows], xg[k, pl.ds(s * T, T)]).astype(BF16)
-            for e in range(local):
-                zb[pl.ds(e * M + s * slots, slots)] = z[e * slots:(e + 1) * slots]
-
-        def expert(e):
-            z = zb[pl.ds(e * M, M)]
-            for t in range(2):
-                q = 2 * e + t
-                n = n_shared + 2 * local * k + q
-                slot = unit_wait(n)
-                for j in range(parts):
-                    cols = pl.ds((t * parts + j) * C, C)
-                    old = jnp.where(k > 0, acc[e, :, cols], 0.0)
-                    acc[e, :, cols] = old + dot(z, ring[slot, j])
-                ahead = q + UNITS
-                if ahead < 2 * local:
-                    start_routed(k, ahead, n + UNITS)
-                else:
-                    ahead -= 2 * local
-
-                    @pl.when(k + 1 < K)
-                    def _():
-                        start_routed(k + 1, ahead, n + UNITS)
-
-                    @pl.when(k + 1 == K)
-                    def _():
-                        start_down(ahead // (local + 2), ahead % (local + 2), n + UNITS)
-
-        for e in range(3):
-            expert(e)
-
-        @pl.when(k + 2 < K)
-        def _():
-            comm_a(k + 2)
-
-        for e in range(3, local):
-            expert(e)
-
-        @pl.when(k + 1 < K)
-        def _():
-            comm_b(k + 1)
-        return 0
-
-    lax.fori_loop(0, K, routed_step, 0)
-    for k in range(K - 2, K):
-        ag_sent(range(9), k)
-
-    for e in range(local):
+    def hidden(e):
         for j in range(parts):
             g = acc[e, :, pl.ds(j * C, C)]
             u = acc[e, :, pl.ds((parts + j) * C, C)]
             xg[6 + j, pl.ds(e * M, M)] = (jax.nn.silu(g) * u).astype(BF16)
+
+    groups = [list(range(e, min(e + 2, local))) for e in range(0, local, 2)]
+
+    def routed_step(k, last):
+        base = n_shared + 2 * local * k
+        ag_wait((2, 5, 6, 7, 8), k)
+        for group in groups:
+            units = [2 * e + t for e in group for t in range(2)]
+            held = [unit_wait(base + q) for q in units]
+            if group[0] == 0:
+                for s in range(members):
+                    z = dot(dm[s, :rows], xg[k, pl.ds(s * T, T)]).astype(BF16)
+                    for e in range(local):
+                        zb[pl.ds(e * M + s * slots, slots)] = z[e * slots:(e + 1) * slots]
+            elif last:
+                hidden(group[0] - 1)
+            for e in group:
+                z = zb[pl.ds(e * M, M)]
+                for t in range(2):
+                    for j in range(parts):
+                        cols = pl.ds((t * parts + j) * C, C)
+                        old = acc[e, :, cols]
+                        if not last:
+                            old = jnp.where(k > 0, old, 0.0)
+                        acc[e, :, cols] = old + dot(z, ring[held[units.index(2 * e + t)], j])
+                if last and e != group[-1]:
+                    hidden(e)
+            for q in units:
+                ahead = q + UNITS
+                if ahead < 2 * local:
+                    start_routed(k, ahead, base + q + UNITS)
+                elif not last:
+                    start_routed(k + 1, ahead - 2 * local, base + q + UNITS)
+                else:
+                    ahead -= 2 * local
+                    start_down(ahead // (local + 2), ahead % (local + 2), base + q + UNITS)
+            if group is groups[1] and not last:
+                @pl.when(k + 2 < K)
+                def _():
+                    comm_a(k + 2)
+        if not last:
+            comm_b(k + 1)
+        return 0
+
+    lax.fori_loop(0, K - 1, lambda k, _: routed_step(k, False), 0)
+    ag_sent(range(9), K - 2)
+    routed_step(K - 1, True)
+    hidden(groups[-1][-1])
+    ag_sent(range(9), K - 1)
 
     spans = ((0, T), (T, T), (2 * T, T), (3 * T, T), (4 * T, H), (4 * T + H, H), (5 * T, T), (6 * T, T))
     targets = (mate, mate, mate, mate, xnbr, ynbr, xnbr, ynbr)
@@ -286,23 +289,29 @@
     def compute(k):
         base = n_shared + n_routed + (local + 2) * k
 
-        def refill(m):
-            ahead = m + UNITS
-            ks, ms = ahead // (local + 2), ahead % (local + 2)
-
-            @pl.when(k + ks < K)
+        def refill(ms):
+            @pl.when(k + 1 < K)
             def _():
-                start_down(k + ks, ms, base + m + UNITS)
-
-        for e in range(local):
-            slot = unit_wait(base + e)
-            out = dot(xg[6, pl.ds(e * M, M)], ring[slot, 0])
-            for j in range(1, parts):
-                out = out + dot(xg[6 + j, pl.ds(e * M, M)], ring[slot, j])
-            out = out.astype(BF16)
-            for s in range(members):
-                zb[pl.ds(s * T + e * slots, slots)] = out[s * slots:(s + 1) * slots]
-            refill(e)
+                for m in ms:
+                    ahead = m + UNITS
+                    if ahead < 2 * (local + 2):
+                        start_down(k + 1, ahead - (local + 2), base + ahead)
+
+            if ms[-1] + UNITS >= 2 * (local + 2):
+                @pl.when(k + 2 < K)
+                def _():
+                    start_down(k + 2, ms[-1] + UNITS - 2 * (local + 2), base + ms[-1] + UNITS)
+
+        for group in (range(3), range(3, local)):
+            held = [unit_wait(base + e) for e in group]
+            for slot, e in zip(held, group):
+                out = dot(xg[6, pl.ds(e * M, M)], ring[slot, 0])
+                for j in range(1, parts):
+                    out = out + dot(xg[6 + j, pl.ds(e * M, M)], ring[slot, j])
+                out = out.astype(BF16)
+                for s in range(members):
+                    zb[pl.ds(s * T + e * slots, slots)] = out[s * slots:(s + 1) * slots]
+            refill(group)
         rs_free(range(4), k)
         for r in range(4):
             s = theirs[r]
@@ -317,15 +326,14 @@
         xg[4 + k % 2, pl.ds(4 * T, T)] = (part(0, k)[...] + got(0, k)).astype(BF16)
         rs_copy(4, k).start()
         rs_copy(5, k).start()
+        held = [unit_wait(base + local + half) for half in range(2)]
         total = None
         for half in range(2):
-            slot = unit_wait(base + local + half)
             for j in range(parts):
-                term = dot(hs[half * parts + j], ring[slot, j])
+                term = dot(hs[half * parts + j], ring[held[half], j])
                 total = term if total is None else total + term
-            if half == 1:
-                part(4, k)[...] = total
-            refill(local + half)
+        part(4, k)[...] = total
+        refill((local, local + 1))
 
     def pass_on(k):
         for kind in (1, 2, 4, 5):
@@ -384,14 +392,10 @@
     members = mesh.shape["ep"]
 
     def body(x, expert, slot, gate, w_gate, w_up, w_down, s_gate, s_up, s_down):
-        x, expert, slot, gate = x[0, 0], expert[0, 0], slot[0, 0], gate[0, 0]
         local, depth, width = w_gate.shape
-        tokens, top = expert.shape
+        tokens, top = expert.shape[2:]
+        x, (expert, slot, gate) = x[0, 0], (jnp.transpose(v[0], (2, 0, 1)) for v in (expert, slot, gate))
         slots = 5 * tokens * top // (4 * members * local)
-        code = jnp.where(slot < slots, expert * slots + slot, -1).astype(F32)
-        weight = gate.astype(BF16).astype(F32)
-        pad = jnp.zeros((8 - top, tokens), F32)
-        pk = jnp.concatenate([code.T, pad, weight.T, pad])
         chunks, parts = depth // C, width // C
         dims = (members, local, slots, top, chunks, parts)
         rows, M = local * slots, members * slots
@@ -400,7 +404,7 @@
         out = pl.pallas_call(
             functools.partial(moe_kernel, dims),
             out_shape=jax.ShapeDtypeStruct((tokens, depth), BF16),
-            in_specs=[pl.BlockSpec(memory_space=pltpu.VMEM)] + [anywhere] * 7,
+            in_specs=[pl.BlockSpec(memory_space=pltpu.VMEM)] * 3 + [anywhere] * 7,
             out_specs=anywhere,
             scratch_shapes=[
                 pltpu.VMEM((chunks, members * tokens, C), BF16),
@@ -411,6 +415,7 @@
                 pltpu.VMEM((members, tokens, tokens), BF16),
                 pltpu.VMEM((members, tokens, tokens), BF16),
                 pltpu.VMEM((members, 16, tokens), F32),
+                pltpu.VMEM((16, tokens), F32),
                 dma((chunks,)), dma((members,)), dma((members,)),
                 dma((9, chunks)), dma((9, chunks)), dma((UNITS,)),
                 dma((8, 2)), dma((8, 4)), dma((2,)),
@@ -419,7 +424,7 @@
                 collective_id=0, has_side_effects=True, vmem_limit_bytes=67_000_000
             ),
             name="moe",
-        )(pk, x, w_gate, w_up, w_down, s_gate, s_up, s_down)
+        )(expert, slot, gate, x, w_gate, w_up, w_down, s_gate, s_up, s_down)
         return out[None, None]
 
     own = P("dp", "ep", None, None)

time: 240 us -> 220 us (0.917)
  Pallas kernels: 234 us -> 217 us
    pallas_call x1, Pallas kernels: 234 us -> 217 us  [body(): pl.pallas_call(functools.partial(moe_kernel, dims), out_shape=jax.ShapeDt...]
where the time goes in v3:
time: 220 us
  Pallas kernels  217 us (99%)
  local copies, waits for them, and re-layouts  3.4 us (2%)
    pallas_call x1, Pallas kernels, body(): pl.pallas_call(functools.partial(moe_kernel, dims), out_shape=jax.ShapeDt...  217 us

profile of v3, /device:TPU:0, one launch (start us, length us, event | category | flops | bytes accessed | tf_op | source)
XLA Modules:
  0.0 220.0 jit_solution(5553347100355729942)
XLA Ops:
  0.0 216.6 %moe.1 = bf16[256,5120]{1,0:T(8,128)(2,1)} custom-call(s32[6,1,256]{2,1,0:T(1,128)} %bitcast.13, s32[6,1,256]{2,1,0:T(1,128)} %bitcast.14, f32[6,1,256]{2,1,0:T(1,128)} %bitcast.15, bf16[256,5120]{1,0:T(8,128)(2,1)} %bitcast.12, bf16[5,5120,1536]{2,1,0:T(8,128)(2,1)} %wg.1, bf16[5,5120,1536]{2,1,0:T(8,128)(2,1)} %wu.1, bf16[5,1536,5120]{2,1,0:T(8,128)(2,1)} %wd.1, ...), custom_call_target="tpu_custom_call" | custom-call | tf_op jit(solution)/shard_map/moe/pallas_call | solution.py:404
  216.6 3.4 %copy.12 = bf16[1,1,256,5120]{3,2,1,0:T(8,128)(2,1)} copy(bf16[1,1,256,5120]{3,2,1,0:T(8,128)(2,1)} %bitcast.11) | data formatting | bytes 5242880

commit v4 on v3

--- a/solution.py
+++ b/solution.py
@@ -31,7 +31,8 @@
     core, yy, xx = me % 2, (me // 2) % 2, me // 4
     mate, ynbr, xnbr = me + 1 - 2 * core, me + 2 - 4 * yy, me + 4 - 8 * xx
     diag = ynbr + 4 - 8 * xx
-    n_shared, n_routed, n_down = 4 * K, 2 * local * K, (local + 2) * K
+    n_shared, n_routed, per_down = 2 * K, 2 * local * K, local + 1
+    half = pl.multiple_of(core * parts * C, C)
 
     def unit_copy(src, r0, c0, down, n):
         slot = n % UNITS
@@ -40,15 +41,15 @@
                 piece = src.at[pl.ds(r0 + j * C, C), pl.ds(c0, C)]
             else:
                 piece = src.at[pl.ds(r0, C), pl.ds(c0 + j * C, C)]
-            pltpu.make_async_copy(piece, ring.at[slot, j], ring_sem.at[slot]).start()
+            pltpu.make_async_copy(piece, ring.at[slot, j], ring_sem.at[slot]).start(priority=1)
 
     def unit_wait(n):
         slot = n % UNITS
         pltpu.make_async_copy(ring.at[slot], ring.at[slot], ring_sem.at[slot]).wait()
         return slot
 
-    def start_shared(i, q, n):
-        unit_copy(sg if q % 2 == 0 else su, pl.multiple_of(i * C, C), (q // 2) * parts * C, False, n)
+    def start_shared(i, t, n):
+        unit_copy((sg, su)[t], pl.multiple_of(i * C, C), half, False, n)
 
     def start_routed(k, q, n):
         w = wg if q % 2 == 0 else wu
@@ -59,7 +60,7 @@
         if m < local:
             unit_copy(wd.at[m], 0, c0, True, n)
         else:
-            unit_copy(sd, (m - local) * parts * C, c0, True, n)
+            unit_copy(sd, half, c0, True, n)
 
     def blk(k, s, off=0, n=T):
         return xg.at[k, pl.ds(pl.multiple_of(s * T + off, 128), n)]
@@ -108,7 +109,7 @@
 
         @pl.when(k + 2 < K)
         def _():
-            ag_start((0, 1, 2), k + 2)
+            ag_start((0, 1), k + 2)
 
     def comm_b(k):
         ag_wait((3, 4), k)
@@ -120,7 +121,7 @@
     for k in range(K):
         own_load(k).start()
     for n in range(UNITS):
-        start_shared(n // 4, n % 4, n)
+        start_shared(n // 2, n % 2, n)
     pk[...] = jnp.zeros(pk.shape, F32)
     for j in range(top):
         place = slot_of[j]
@@ -147,49 +148,10 @@
 
     for k in range(2, K):
         own_load(k).wait()
-
-    def shared_step(i, _):
-        xo = blk(i, me)
-        held = [unit_wait(4 * i + q) for q in range(4)]
-        for half in range(2):
-            for t in range(2):
-                for j in range(parts):
-                    cols = pl.ds((t * parts + j) * C, C)
-                    old = jnp.where(i > 0, acc[3 + half, :T, cols], 0.0)
-                    acc[3 + half, :T, cols] = old + dot(xo[...], ring[held[2 * half + t], j])
-
-        @pl.when(i < K - 2)
-        def _():
-            for q in range(4):
-                start_shared(i + 2, q, 4 * i + q + UNITS)
-
-        for late in range(2):
-            @pl.when(i == K - 2 + late)
-            def _():
-                for q in range(4):
-                    start_routed(0, 4 * late + q, 4 * i + q + UNITS)
-
-        @pl.when(i == 3)
-        def _():
-            comm_a(0)
-
-        @pl.when(i == 7)
-        def _():
-            comm_a(1)
-        return 0
-
-    lax.fori_loop(0, K, shared_step, 0)
-    for half in range(2):
-        for j in range(parts):
-            g = acc[3 + half, :T, pl.ds(j * C, C)]
-            u = acc[3 + half, :T, pl.ds((parts + j) * C, C)]
-            hs[half * parts + j] = (jax.nn.silu(g) * u).astype(BF16)
-
+        ag_start((2,), k)
     zb[pl.ds(local * M, members * T - local * M)] = jnp.zeros((members * T - local * M, C), BF16)
-    for d in range(1, members):
-        code_copy(d, pk, cg.at[(me + members - d) % members], mate).wait_recv()
-
-    def tables(s, _):
+
+    def tables(s):
         codes = cg[s]
         row = lax.broadcasted_iota(jnp.int32, (T, T), 0)
         row = jnp.where(row < rows, row + me * rows, -2).astype(F32)
@@ -201,9 +163,53 @@
             weight = jnp.where(same, codes[8 + j:9 + j, :], weight)
         dm[s] = hit.astype(BF16)
         wm[s] = weight.T.astype(BF16)
+
+    def shared_step(i, _):
+        ag_wait((2,), i)
+        held = [unit_wait(2 * i + t) for t in range(2)]
+        both = xg[i, pl.ds(pl.multiple_of((me - core) * T, 2 * T), 2 * T)]
+        for t in range(2):
+            for j in range(parts):
+                cols = pl.ds((t * parts + j) * C, C)
+                term = dot(both, ring[held[t], j])
+                acc[3, :T, cols] = jnp.where(i > 0, acc[3, :T, cols], 0.0) + term[:T]
+                acc[4, :T, cols] = jnp.where(i > 0, acc[4, :T, cols], 0.0) + term[T:]
+
+        @pl.when(i < K - 4)
+        def _():
+            for t in range(2):
+                start_shared(i + 4, t, 2 * i + t + UNITS)
+
+        for late in range(4):
+            @pl.when(i == K - 4 + late)
+            def _():
+                for t in range(2):
+                    start_routed(0, 2 * late + t, 2 * i + t + UNITS)
+
+        @pl.when(i == 1)
+        def _():
+            for d in range(1, members):
+                code_copy(d, pk, cg.at[(me + members - d) % members], mate).wait_recv()
+
+        @pl.when(i >= 2)
+        def _():
+            tables(i - 2)
+
+        @pl.when(i == 4)
+        def _():
+            comm_a(0)
+
+        @pl.when(i == 8)
+        def _():
+            comm_a(1)
         return 0
 
-    lax.fori_loop(0, members, tables, 0)
+    lax.fori_loop(0, K, shared_step, 0)
+    for side in range(2):
+        for j in range(parts):
+            g = acc[3 + side, :T, pl.ds(j * C, C)]
+            u = acc[3 + side, :T, pl.ds((parts + j) * C, C)]
+            hs[j, pl.ds(side * T, T)] = (jax.nn.silu(g) * u).astype(BF16)
     comm_b(0)
 
     def hidden(e):
@@ -212,11 +218,11 @@
             u = acc[e, :, pl.ds((parts + j) * C, C)]
             xg[6 + j, pl.ds(e * M, M)] = (jax.nn.silu(g) * u).astype(BF16)
 
-    groups = [list(range(e, min(e + 2, local))) for e in range(0, local, 2)]
+    groups = [[0], list(range(1, local - 2)), [local - 2], [local - 1]]
 
     def routed_step(k, last):
         base = n_shared + 2 * local * k
-        ag_wait((2, 5, 6, 7, 8), k)
+        ag_wait((5, 6, 7, 8), k)
         for group in groups:
             units = [2 * e + t for e in group for t in range(2)]
             held = [unit_wait(base + q) for q in units]
@@ -246,13 +252,13 @@
                     start_routed(k + 1, ahead - 2 * local, base + q + UNITS)
                 else:
                     ahead -= 2 * local
-                    start_down(ahead // (local + 2), ahead % (local + 2), base + q + UNITS)
+                    start_down(ahead // per_down, ahead % per_down, base + q + UNITS)
             if group is groups[1] and not last:
                 @pl.when(k + 2 < K)
                 def _():
                     comm_a(k + 2)
-        if not last:
-            comm_b(k + 1)
+            if group is groups[2] and not last:
+                comm_b(k + 1)
         return 0
 
     lax.fori_loop(0, K - 1, lambda k, _: routed_step(k, False), 0)
@@ -287,53 +293,58 @@
         return acc.at[k % 4, pl.ds(0, T), pl.ds(r * C, C)]
 
     def compute(k):
-        base = n_shared + n_routed + (local + 2) * k
+        base = n_shared + n_routed + per_down * k
 
         def refill(ms):
-            @pl.when(k + 1 < K)
-            def _():
-                for m in ms:
-                    ahead = m + UNITS
-                    if ahead < 2 * (local + 2):
-                        start_down(k + 1, ahead - (local + 2), base + ahead)
-
-            if ms[-1] + UNITS >= 2 * (local + 2):
-                @pl.when(k + 2 < K)
-                def _():
-                    start_down(k + 2, ms[-1] + UNITS - 2 * (local + 2), base + ms[-1] + UNITS)
-
-        for group in (range(3), range(3, local)):
-            held = [unit_wait(base + e) for e in group]
+            for ks in (1, 2):
+                some = [m for m in ms if (m + UNITS) // per_down == ks]
+                if some:
+                    @pl.when(k + ks < K)
+                    def _():
+                        for m in some:
+                            start_down(k + ks, (m + UNITS) % per_down, base + m + UNITS)
+
+        for group in (range(3), range(3, per_down)):
+            held = [unit_wait(base + m) for m in group]
             for slot, e in zip(held, group):
+                if e == local:
+                    continue
                 out = dot(xg[6, pl.ds(e * M, M)], ring[slot, 0])
                 for j in range(1, parts):
                     out = out + dot(xg[6 + j, pl.ds(e * M, M)], ring[slot, j])
                 out = out.astype(BF16)
                 for s in range(members):
                     zb[pl.ds(s * T + e * slots, slots)] = out[s * slots:(s + 1) * slots]
-            refill(group)
-        rs_free(range(4), k)
-        for r in range(4):
-            s = theirs[r]
-            p = dot(wm[s], zb[pl.ds(pl.multiple_of(s * T, T), T)])
+            refill([m for m in group if m < local])
+        shared = held[-1]
+
+        def combined(s):
+            return dot(wm[s], zb[pl.ds(pl.multiple_of(s * T, T), T)])
+
+        def shared_part(side):
+            total = None
+            for j in range(parts):
+                term = dot(hs[j, pl.ds(pl.multiple_of(side * T, T), T)], ring[shared, j])
+                total = term if total is None else total + term
+            return total
+
+        def send(r, p):
             xg[4 + k % 2, pl.ds(r * T, T)] = p.astype(BF16)
             rs_copy(r, k).start()
-        for r in range(4):
-            s = mine[r]
-            part(r, k)[...] = dot(wm[s], zb[pl.ds(pl.multiple_of(s * T, T), T)])
+
+        rs_free(range(4), k)
+        for r in range(3):
+            send(r, combined(theirs[r]))
+        for r in range(3):
+            part(r, k)[...] = combined(mine[r])
         rs_copy(0, k).wait_recv()
         rs_free((4, 5), k)
         xg[4 + k % 2, pl.ds(4 * T, T)] = (part(0, k)[...] + got(0, k)).astype(BF16)
         rs_copy(4, k).start()
         rs_copy(5, k).start()
-        held = [unit_wait(base + local + half) for half in range(2)]
-        total = None
-        for half in range(2):
-            for j in range(parts):
-                term = dot(hs[half * parts + j], ring[held[half], j])
-                total = term if total is None else total + term
-        part(4, k)[...] = total
-        refill((local, local + 1))
+        send(3, combined(theirs[3]) + shared_part(1 - core))
+        part(3, k)[...] = combined(mine[3]) + shared_part(core)
+        refill([local])
 
     def pass_on(k):
         for kind in (1, 2, 4, 5):
@@ -361,7 +372,7 @@
         def _():
             out_copy(k - 2).wait()
 
-        total = part(3, k)[...] + got(3, k) + got(6, k) + got(7, k) + part(4, k)[...]
+        total = part(3, k)[...] + got(3, k) + got(6, k) + got(7, k)
         xg[9, pl.ds((k % 2) * T, T)] = total.astype(BF16)
         out_copy(k).start()
 
@@ -410,7 +421,7 @@
                 pltpu.VMEM((chunks, members * tokens, C), BF16),
                 pltpu.VMEM((local, M, 2 * width), F32),
                 pltpu.VMEM((UNITS, parts, C, C), BF16),
-                pltpu.VMEM((2 * parts, tokens, C), BF16),
+                pltpu.VMEM((parts, 2 * tokens, C), BF16),
                 pltpu.VMEM((members * tokens, C), BF16),
                 pltpu.VMEM((members, tokens, tokens), BF16),
                 pltpu.VMEM((members, tokens, tokens), BF16),

time: 220 us -> 214 us (0.973)
  Pallas kernels: 217 us -> 210 us
    pallas_call x1, Pallas kernels: 217 us -> 210 us  [body(): pl.pallas_call(functools.partial(moe_kernel, dims), out_shape=jax.ShapeDt...]
where the time goes in v4:
time: 214 us; the launch traced here: 213 us
  Pallas kernels  210 us (98%)
  local copies, waits for them, and re-layouts  3.4 us (2%)
    pallas_call x1, Pallas kernels, body(): pl.pallas_call(functools.partial(moe_kernel, dims), out_shape=jax.ShapeDt...  210 us

profile of v4, /device:TPU:0, one launch (start us, length us, event | category | flops | bytes accessed | tf_op | source)
XLA Modules:
  0.0 213.4 jit_solution(14061477313967085072)
XLA Ops:
  0.0 210.0 %moe.1 = bf16[256,5120]{1,0:T(8,128)(2,1)} custom-call(s32[6,1,256]{2,1,0:T(1,128)} %bitcast.13, s32[6,1,256]{2,1,0:T(1,128)} %bitcast.14, f32[6,1,256]{2,1,0:T(1,128)} %bitcast.15, bf16[256,5120]{1,0:T(8,128)(2,1)} %bitcast.12, bf16[5,5120,1536]{2,1,0:T(8,128)(2,1)} %wg.1, bf16[5,5120,1536]{2,1,0:T(8,128)(2,1)} %wu.1, bf16[5,1536,5120]{2,1,0:T(8,128)(2,1)} %wd.1, ...), custom_call_target="tpu_custom_call" | custom-call | tf_op jit(solution)/shard_map/moe/pallas_call | solution.py:415
  210.0 3.4 %copy.12 = bf16[1,1,256,5120]{3,2,1,0:T(8,128)(2,1)} copy(bf16[1,1,256,5120]{3,2,1,0:T(8,128)(2,1)} %bitcast.11) | data formatting | bytes 5242880

commit v5 on v4

--- a/solution.py
+++ b/solution.py
@@ -195,11 +195,11 @@
         def _():
             tables(i - 2)
 
-        @pl.when(i == 4)
+        @pl.when(i == 3)
         def _():
             comm_a(0)
 
-        @pl.when(i == 8)
+        @pl.when(i == 7)
         def _():
             comm_a(1)
         return 0
@@ -218,7 +218,7 @@
             u = acc[e, :, pl.ds((parts + j) * C, C)]
             xg[6 + j, pl.ds(e * M, M)] = (jax.nn.silu(g) * u).astype(BF16)
 
-    groups = [[0], list(range(1, local - 2)), [local - 2], [local - 1]]
+    groups = [[0], list(range(1, local - 2)), [local - 2, local - 1]]
 
     def routed_step(k, last):
         base = n_shared + 2 * local * k
@@ -253,11 +253,11 @@
                 else:
                     ahead -= 2 * local
                     start_down(ahead // per_down, ahead % per_down, base + q + UNITS)
-            if group is groups[1] and not last:
+            if group is groups[0] and not last:
                 @pl.when(k + 2 < K)
                 def _():
                     comm_a(k + 2)
-            if group is groups[2] and not last:
+            if group is groups[1] and not last:
                 comm_b(k + 1)
         return 0
 

time: 214 us -> 211 us (0.986)
    pallas_call x1, Pallas kernels: 210 us -> 208 us  [body(): pl.pallas_call(functools.partial(moe_kernel, dims), out_shape=jax.ShapeDt...]
where the time goes in v5:
time: 211 us
  Pallas kernels  208 us (99%)
  local copies, waits for them, and re-layouts  3.4 us (2%)
    pallas_call x1, Pallas kernels, body(): pl.pallas_call(functools.partial(moe_kernel, dims), out_shape=jax.ShapeDt...  208 us

profile of v5, /device:TPU:0, one launch (start us, length us, event | category | flops | bytes accessed | tf_op | source)
XLA Modules:
  0.0 211.2 jit_solution(2891445615999423261)
XLA Ops:
  0.0 207.8 %moe.1 = bf16[256,5120]{1,0:T(8,128)(2,1)} custom-call(s32[6,1,256]{2,1,0:T(1,128)} %bitcast.13, s32[6,1,256]{2,1,0:T(1,128)} %bitcast.14, f32[6,1,256]{2,1,0:T(1,128)} %bitcast.15, bf16[256,5120]{1,0:T(8,128)(2,1)} %bitcast.12, bf16[5,5120,1536]{2,1,0:T(8,128)(2,1)} %wg.1, bf16[5,5120,1536]{2,1,0:T(8,128)(2,1)} %wu.1, bf16[5,1536,5120]{2,1,0:T(8,128)(2,1)} %wd.1, ...), custom_call_target="tpu_custom_call" | custom-call | tf_op jit(solution)/shard_map/moe/pallas_call | solution.py:415
  207.8 3.4 %copy.12 = bf16[1,1,256,5120]{3,2,1,0:T(8,128)(2,1)} copy(bf16[1,1,256,5120]{3,2,1,0:T(8,128)(2,1)} %bitcast.11) | data formatting | bytes 5242880
